TPU v7x, 32 devices: a whole 2x2x4 slice. The times are simulated.
32 devices in a mesh: grp: 2 (over y), seq: 4 (over z), head: 2 (over x), rep: 2 (over core).
Axes of the slice: x: 2, y: 2, z: 4, core: 2. Of those that a mesh axis runs over, the one named last changes fastest.
Arguments:
- x_proj: bfloat16 [4, 4, 4, 32, 8192], P(('grp', 'rep'), None, 'seq', None, 'head'), parts along dimension 0, may hold values from -6 to 6
- gate_proj: bfloat16 [4, 4, 4, 32, 8192], P(('grp', 'rep'), None, 'seq', None, 'head'), parts along dimension 0, may hold values from -6 to 6
- bc_proj: bfloat16 [4, 4, 4, 32, 256], P(('grp', 'rep'), None, 'seq'), parts along dimension 0, may hold values from -6 to 6
- dt_proj: bfloat16 [4, 4, 4, 32, 128], P(('grp', 'rep'), None, 'seq', None, 'head'), parts along dimension 0, may hold values from -5.5 to 7.5
- a_rate: float32 [128], P('head'), may hold values from 0.0001953125 to 0.05
- dt_bias: float32 [128], P('head'), may hold values from -1 to 1
- d_skip: float32 [128], P('head'), may hold values from 0.5 to 1.5
- conv_x_weight: float32 [4, 8192], P(None, 'head'), may hold values from -3 to 3
- conv_bc_weight: float32 [4, 256], replicated, may hold values from -3 to 3
- norm_gain: float32 [8192], P('head'), may hold values from 0.1 to 1.9
- out_weight: bfloat16 [8192, 2048], P(('seq', 'rep'), 'head'), may hold values from -0.0625 to 0.0625
- request_first_position: int32 [4], P(('grp', 'rep')), parts along dimension 0, may hold values from 0 to 255
- owner: int32 [4, 4], P(('grp', 'rep')), parts along dimension 0, may hold values from 0 to 3, each once within a row
Outputs:
- mixed: bfloat16 [4, 512, 2048], P(('grp', 'rep'), 'seq', 'head'), parts along dimension 0
- ssm_state: float32 [4, 4, 128, 2048], P(('grp', 'rep'), 'seq', 'head'), parts along dimension 0
- conv_x_state: bfloat16 [4, 4, 3, 2048], P(('grp', 'rep'), 'seq', None, 'head'), parts along dimension 0
- conv_bc_state: bfloat16 [4, 4, 3, 64], P(('grp', 'rep'), 'seq'), parts along dimension 0
There are 2 independent parts, one for each index of `grp`. A program takes and returns all parts, laid end to end along the dimension named above; an argument that names none is the same for every part. Nothing has to cross between parts.
Inputs may be any that keep to these rules, and one draw needn't show every extreme that they name: Each row of owner names every index of seq once.
All inputs are finite; a program needn't handle non-finite values.
Results may differ from a plain program's by a relative error of at most 0.007.
Values may be sent and summed in bfloat16 or wider, within the bound.
A program may use at most 128 MiB of HBM per device.

v0:
```python
import jax
import jax.numpy as jnp
from jax import lax
from jax.sharding import PartitionSpec as P

HEAD_DIM = 64
NSTATE = 128
KCONV = 4
SPAN = 128
INNER = 8192
highest = lax.Precision.HIGHEST
stability_constant = 1e-05


def passed_along(value, axis, by):
    devices = lax.axis_size(axis)
    pairs = [(i, i + by) for i in range(devices) if 0 <= i + by < devices]
    return lax.ppermute(value, axis, pairs)


def prefix(value, axis, combine, identity, reverse):
    devices, place = (lax.axis_size(axis), lax.axis_index(axis))
    everything = jax.tree.map(lambda part: lax.all_gather(part, axis), value)
    start = jax.tree.map(
        lambda part, zero: jnp.broadcast_to(jnp.asarray(zero, part.dtype), part.shape),
        value,
        identity,
    )

    def lap(k, before):
        at = devices - 1 - k if reverse else k
        reached = at > place if reverse else at < place
        new = combine(before, jax.tree.map(lambda part: part[at], everything))
        return jax.tree.map(lambda a, b: jnp.where(reached, a, b), new, before)

    return lax.fori_loop(0, devices, lap, start)


def broadcast(block, axis, source):
    block = jnp.where(lax.axis_index(axis) == source, block, jnp.zeros_like(block))
    return lax.psum(block, axis)


def span_terms(x_conv, b_rows, c_rows, step_size, log_decay):
    cum_decay = jnp.cumsum(log_decay, axis=1)
    scores = jnp.einsum("kqn,ktn->kqt", c_rows, b_rows, preferred_element_type=jnp.float32)
    cum_heads = jnp.swapaxes(cum_decay, 1, 2)
    step_heads = jnp.swapaxes(step_size, 1, 2)
    block_len = cum_decay.shape[1]
    causal = jnp.arange(block_len)[:, None] >= jnp.arange(block_len)[None, :]
    decay_gap = cum_heads[:, :, :, None] - cum_heads[:, :, None, :]
    seg_decay = jnp.exp(jnp.where(causal, decay_gap, -jnp.inf))
    weights = (scores[:, None] * seg_decay * step_heads[:, :, None, :]).astype(jnp.bfloat16)
    y_intra = jnp.einsum("khqt,kthp->kqhp", weights, x_conv, preferred_element_type=jnp.float32)
    remaining_length = jnp.exp(cum_decay[:, -1:, :] - cum_decay)
    scaled = ((remaining_length * step_size)[..., None] * x_conv.astype(jnp.float32)).astype(
        jnp.bfloat16
    )
    states = jnp.einsum("kthp,ktn->khpn", scaled, b_rows, preferred_element_type=jnp.float32)
    return (cum_decay, y_intra, states, jnp.exp(cum_decay[:, -1, :]))


def conv_silu(preceding_tokens, current, weight):
    extended = jnp.concatenate([preceding_tokens, current], axis=0)
    length = current.shape[0]
    accum = jnp.zeros(current.shape, jnp.float32)
    for offset in range(weight.shape[0]):
        accum = accum + weight[offset] * extended[offset : offset + length].astype(jnp.float32)
    return jax.nn.silu(accum)


def link(preceding_tokens, later):
    return (
        preceding_tokens[0] * later[0],
        later[0][:, None, None] * preceding_tokens[1] + later[1],
    )


def multiply(preceding_tokens, later):
    return preceding_tokens * later


def add_rows(source, piece):
    return jnp.dot(source, piece, preferred_element_type=jnp.float32)


def take_slab(values, slab_index, seq_count):
    grouped = values.reshape(values.shape[0], seq_count, -1)
    return lax.dynamic_index_in_dim(grouped, slab_index, axis=1, keepdims=False)


def local(
    x_proj,
    gate_proj,
    bc_proj,
    dt_proj,
    a_rate,
    dt_bias,
    d_skip,
    conv_x_weight,
    conv_bc_weight,
    norm_gain,
    out_weight,
    request_first_position,
    owner,
):
    x_all, z_all, bc_all, dt_all = (
        lax.all_to_all(x_proj, "seq", split_axis=1, concat_axis=2, tiled=True),
        lax.all_to_all(gate_proj, "seq", split_axis=1, concat_axis=2, tiled=True),
        lax.all_to_all(bc_proj, "seq", split_axis=1, concat_axis=2, tiled=True),
        lax.all_to_all(dt_proj, "seq", split_axis=1, concat_axis=2, tiled=True),
    )
    tokens_here = x_all.shape[2] * x_all.shape[3]
    x_local = x_all.reshape(tokens_here, x_all.shape[4])
    z_local = z_all.reshape(tokens_here, z_all.shape[4])
    bc_local = bc_all.reshape(tokens_here, bc_all.shape[4])
    dt_local = dt_all.reshape(tokens_here, dt_all.shape[4])
    heads = dt_local.shape[1]
    seq_index = lax.axis_index("seq")
    seq_count = lax.axis_size("seq")
    positions = seq_index * tokens_here + jnp.arange(tokens_here, dtype=jnp.int32)
    is_live = positions >= request_first_position[0]
    x_live = jnp.where(is_live[:, None], x_local, jnp.zeros_like(x_local))
    bc_live = jnp.where(is_live[:, None], bc_local, jnp.zeros_like(bc_local))
    rim_rows = KCONV - 1
    tail_x = x_live[tokens_here - rim_rows :]
    tail_bc = bc_live[tokens_here - rim_rows :]
    before_x, before_bc = passed_along((tail_x, tail_bc), "seq", 1)
    x_conv = conv_silu(before_x, x_live, conv_x_weight).astype(jnp.bfloat16)
    bc_conv = conv_silu(before_bc, bc_live, conv_bc_weight).astype(jnp.bfloat16)
    step_size = (
        jax.nn.softplus(dt_local.astype(jnp.float32) + dt_bias)
        * is_live.astype(jnp.float32)[:, None]
    )
    log_decay = -a_rate * step_size
    blocks = tokens_here // SPAN
    x_blocks = x_conv.reshape(blocks, SPAN, heads, HEAD_DIM)
    b_blocks = bc_conv[:, :NSTATE].reshape(blocks, SPAN, NSTATE)
    c_blocks = bc_conv[:, NSTATE:].reshape(blocks, SPAN, NSTATE)
    cum_decay, y_intra, states, decays = span_terms(
        x_blocks,
        b_blocks,
        c_blocks,
        step_size.reshape(blocks, SPAN, heads),
        log_decay.reshape(blocks, SPAN, heads),
    )

    def advance(carry, inputs):
        factor, contrib = inputs
        return (factor[:, None, None] * carry + contrib, carry)

    zero_state = jnp.zeros((heads, HEAD_DIM, NSTATE), jnp.float32)
    local_final, local_enter = lax.scan(advance, zero_state, (decays, states))
    dev_decay = jnp.prod(decays, axis=0)
    ones_heads = jnp.ones((heads,), jnp.float32)
    enter_decay, enter_state = prefix(
        (dev_decay, local_final), "seq", link, (ones_heads, zero_state), False
    )
    c_wide = c_blocks.astype(jnp.float32)
    before_block = jnp.concatenate([ones_heads[None], jnp.cumprod(decays, axis=0)[:-1]], axis=0)
    entering = local_enter + before_block[:, :, None, None] * enter_state[None]
    y_state = jnp.exp(cum_decay)[..., None] * jnp.einsum(
        "kqn,khpn->kqhp", c_wide, entering, precision=highest
    )
    y_total = y_intra + y_state + d_skip[:, None] * x_blocks.astype(jnp.float32)
    y_flat = y_total.reshape(tokens_here, heads * HEAD_DIM)
    gated = y_flat * jax.nn.silu(z_local.astype(jnp.float32))
    square_sums = lax.psum(jnp.sum(gated * gated, axis=1), "head")
    normed = (
        gated * lax.rsqrt(square_sums[:, None] / INNER + stability_constant) * norm_gain
    ).astype(jnp.bfloat16)
    last_index = seq_count - 1
    after_decay = prefix(dev_decay, "seq", multiply, ones_heads, True)
    final_state = lax.psum(after_decay[:, None, None] * local_final, "seq")
    keep_x, keep_bc = (broadcast(tail_x, "seq", last_index), broadcast(tail_bc, "seq", last_index))
    slab_index = jnp.sum(
        jnp.where(owner[0] == seq_index, jnp.arange(seq_count, dtype=jnp.int32), 0)
    )
    ssm_state = take_slab(final_state.reshape(heads, -1), slab_index, seq_count)[None, None]
    conv_x_state = take_slab(keep_x, slab_index, seq_count)[None, None]
    conv_bc_state = take_slab(keep_bc, slab_index, seq_count)[None, None]
    features = lax.all_gather(normed, "head", axis=1, tiled=True)
    out_cols = out_weight.shape[1]
    mixed_sum = add_rows(features, lax.all_gather(out_weight, ("seq", "rep"), axis=0, tiled=True))
    mixed = mixed_sum.astype(jnp.bfloat16).reshape(1, tokens_here, out_cols)
    return (mixed, ssm_state, conv_x_state, conv_bc_state)


def solution(mesh):
    return jax.shard_map(
        local,
        mesh=mesh,
        in_specs=(
            P(("grp", "rep"), None, "seq", None, "head"),
            P(("grp", "rep"), None, "seq", None, "head"),
            P(("grp", "rep"), None, "seq", None, None),
            P(("grp", "rep"), None, "seq", None, "head"),
            P("head"),
            P("head"),
            P("head"),
            P(None, "head"),
            P(),
            P("head"),
            P(("seq", "rep"), "head"),
            P(("grp", "rep")),
            P(("grp", "rep"), None),
        ),
        out_specs=(
            P(("grp", "rep"), "seq", "head"),
            P(("grp", "rep"), "seq", "head", None),
            P(("grp", "rep"), "seq", None, "head"),
            P(("grp", "rep"), "seq", None, None),
        ),
        check_vma=False,
    )
```

profile of v0, /device:TPU:0, one launch (start us, length us, event | category | flops | bytes accessed | tf_op | source)
XLA Modules:
  0.0 532.8 jit_solution(8478039113186121479)
XLA Ops:
  8.6 6.3 %all-to-all-start.2 = ((bf16[4,2,1024]{2,1,0:T(2,128)(2,1)}), bf16[4,2,1024]{2,1,0:T(2,128)(2,1)S(1)}, u32[]{:S(2)}, u32[]{:S(2)}) async-start(bf16[4,2,1024]{2,1,0:T(2,128)(2,1)} %reshape.454), calls=%async_computation.2 | async-start | bytes 32768 | tf_op jit(solution)/shard_map/all_to_all | solution.py:111
  20.6 4.5 all-to-all-start.1
  27.1 1.9 copy.80
  29.0 11.5 %all-gather = f32[4,1,64]{2,1,0:T(1,128)S(1)} all-gather(f32[1,1,64]{2,1,0:T(1,128)S(1)} %get-tuple-element.290), channel_id=2, replica_groups=mesh['grp'=2,'seq'=4,'head'=2,'rep'=2] {'seq'}, dimensions={0}, use_global_device_ids=true | all-gather | bytes 1280 | tf_op jit(solution)/shard_map/all_gather | solution.py:23
  40.5 3.7 all-to-all-start
  46.6 3.8 collective-permute-start.1
  50.4 16.6 %all-to-all-done = bf16[1,4,1,32,4096]{4,3,2,0,1:T(8,128)(2,1)S(1)} async-done(((bf16[1,4,1,32,4096]{4,3,2,0,1:T(8,128)(2,1)}), bf16[1,4,1,32,4096]{4,3,2,0,1:T(8,128)(2,1)S(1)}, u32[]{:S(2)}, u32[]{:S(2)}) %all-to-all-start) | async-done | bytes 1048608 | tf_op jit(solution)/shard_map/all_to_all | solution.py:108
  70.2 3.1 multiply_convert_fusion.2
  74.9 2.4 broadcast_multiply_fusion
  77.3 5.7 %all-to-all-start.3 = ((bf16[1,4,1,32,4096]{4,3,2,0,1:T(8,128)(2,1)}), bf16[1,4,1,32,4096]{4,3,2,0,1:T(8,128)(2,1)}, u32[]{:S(2)}, u32[]{:S(2)}) async-start(bf16[1,4,1,32,4096]{4,3,2,0,1:T(8,128)(2,1)} %bitcast.35), calls=%async_computation.3 | async-start | bytes 2097152 | tf_op jit(solution)/shard_map/all_to_all | solution.py:109
  83.5 48.3 %all-to-all-done.3 = bf16[1,4,1,32,4096]{4,3,2,0,1:T(8,128)(2,1)} async-done(((bf16[1,4,1,32,4096]{4,3,2,0,1:T(8,128)(2,1)}), bf16[1,4,1,32,4096]{4,3,2,0,1:T(8,128)(2,1)}, u32[]{:S(2)}, u32[]{:S(2)}) %all-to-all-start.3) | async-done | bytes 1048608 | tf_op jit(solution)/shard_map/all_to_all | solution.py:109
  131.8 2.7 bitcast_convert_fusion
  134.6 4.6 reshape.449
  139.2 4.8 copy.87
  147.0 3.0 reshape_reshape.3
  151.2 3.3 fusion.1
  154.4 87.4 %all-gather.10.cloned.1.call-done = f32[256,64,128]{2,1,0:T(8,128)} async-done(((f32[64,64,128]{2,1,0:T(8,128)}), f32[256,64,128]{2,1,0:T(8,128)}) %all-gather.10.cloned.1.call-update) | async-done | bytes 8388624 | tf_op jit(solution)/shard_map/all_gather | solution.py:23
  241.9 11.4 %while.35 = (s32[]{:T(128)}, f32[64,64,128]{2,1,0:T(8,128)S(1)}, s32[]{:T(128)}, f32[4,64]{1,0:T(4,128)}, f32[4,64,64,128]{3,2,1,0:T(8,128)}, /*index=5*/s32[]{:T(128)}, s32[]{:T(128)}) while((s32[]{:T(128)}, f32[64,64,128]{2,1,0:T(8,128)S(1)}, s32[]{:T(128)}, f32[4,64]{1,0:T(4,128)}, f32[4,64,64,128]{3,2,1,0:T(8,128)}, ...), condition=%wide.region_2.3_spmd.clone, body=%wide.region_1.2_spmd.clone.sunk | while | flops 2097156 | bytes 6292329 | solution.py:36
  242.6 2.1 fusion.44
  245.3 2.1 fusion.44
  248.1 2.3 fusion.44
  251.1 2.1 fusion.44
  253.2 5.9 %multiply_reduce_fusion = (f32[128]{0:T(128)S(1)}, f32[1,128,64,64]{1,3,2,0:T(8,128)}) fusion(f32[1,128,64,64]{1,3,2,0:T(8,128)} %copy.87, f32[1,128,64,64]{1,3,2,0:T(8,128)} %bitcast.133, f32[64]{0:T(128)S(1)} %copy-done.18, f32[64,64,128]{2,1,0:T(8,128)S(1)} %get-tuple-element.223, bf16[128,256]{1,0:T(8,128)(2,1)S(1)} %multiply_convert_fusion.4, ...), kind=kOutput, calls=%fused_computation.17 | convolution fusion | flops 811073408 | bytes 10552320 | tf_op jit(solution)/shard_map/kqn,khpn->kqhp/dot_general | solution.py:162
  259.1 3.1 copy.85
  262.2 4.9 psum.28
  267.1 3.3 fusion.14
  273.7 18.3 %all-reduce = (bf16[3,4,1024]{2,0,1:T(4,128)(2,1)S(1)}, bf16[3,4,64]{2,0,1:T(4,128)(2,1)S(1)}) all-reduce(bf16[3,4,1024]{2,0,1:T(4,128)(2,1)S(1)} %bitcast.140, bf16[3,4,64]{2,0,1:T(4,128)(2,1)S(1)} %copy.89), channel_id=1, replica_groups=mesh['grp'=2,'seq'=4,'head'=2,'rep'=2] {'seq'}, use_global_device_ids=true, to_apply=%region_9.10 | all-reduce | flops 13056 | bytes 52224 | tf_op jit(solution)/shard_map/psum | solution.py:41
  293.2 37.3 %all-reduce.3.cloned.1.call-done = f32[64,4,2048]{2,1,0:T(4,128)} async-done(((f32[64,4,2048]{2,1,0:T(4,128)}), f32[64,4,2048]{2,1,0:T(4,128)}) %all-reduce.3.cloned.1.call-update) | async-done | bytes 2097168 | tf_op jit(solution)/shard_map/psum | solution.py:174
  330.5 2.1 constant_dynamic-slice_fusion
  333.6 30.6 %all-gather.6.cloned.1.call-done = bf16[128,8192]{1,0:T(8,128)(2,1)} async-done(((bf16[128,4096]{1,0:T(8,128)(2,1)}), bf16[128,8192]{1,0:T(8,128)(2,1)}) %all-gather.6.cloned.1.call-update) | async-done | bytes 2097168 | tf_op jit(solution)/shard_map/all_gather | solution.py:182
  364.2 152.6 %all-gather.8.cloned.1.call-done = bf16[8192,1024]{1,0:T(8,128)(2,1)} async-done(((bf16[1024,1024]{1,0:T(8,128)(2,1)}), bf16[8192,1024]{1,0:T(8,128)(2,1)}) %all-gather.8.cloned.1.call-update) | async-done | bytes 16777232 | tf_op jit(solution)/shard_map/all_gather | solution.py:184
  516.8 9.5 %fusion.16 = bf16[1,128,1024]{2,1,0:T(8,128)(2,1)} fusion(bf16[128,8192]{1,0:T(8,128)(2,1)} %all-gather.6.cloned.1.call-done, bf16[8192,1024]{1,0:T(8,128)(2,1)} %all-gather.8.cloned.1.call-done), kind=kOutput, calls=%fused_computation.31 | convolution fusion | flops 2147614720 | bytes 19136512 | tf_op jit(solution)/shard_map/dot_general | solution.py:84
  (99 shorter events, 26.4 us)
Async XLA Ops:
  7.2 0.8 copy-start
  8.6 12.0 %all-to-all-start.2 = ((bf16[4,2,1024]{2,1,0:T(2,128)(2,1)}), bf16[4,2,1024]{2,1,0:T(2,128)(2,1)S(1)}, u32[]{:S(2)}, u32[]{:S(2)}) async-start(bf16[4,2,1024]{2,1,0:T(2,128)(2,1)} %reshape.454), calls=%async_computation.2 | async-start | bytes 32768 | tf_op jit(solution)/shard_map/all_to_all | solution.py:111
  19.3 7.5 %copy-start.11 = (f32[128]{0:T(128)}, f32[128]{0:T(128)S(1)}, u32[]{:S(2)}) copy-start(f32[128]{0:T(128)S(1)} %get-tuple-element.282) | copy-start | bytes 1540
  20.6 19.9 %all-to-all-start.1 = ((bf16[1,4,1,32,256]{4,3,2,0,1:T(8,128)(2,1)}), bf16[1,4,1,32,256]{4,3,2,0,1:T(8,128)(2,1)S(1)}, u32[]{:S(2)}, u32[]{:S(2)}) async-start(bf16[1,4,1,32,256]{4,3,2,0,1:T(8,128)(2,1)} %bitcast.145), calls=%async_computation.1 | async-start | bytes 131072 | tf_op jit(solution)/shard_map/all_to_all | solution.py:110
  29.0 15.8 %copy-start.6 = (f32[64]{0:T(128)S(1)}, f32[64]{0:T(128)}, u32[]{:S(2)}) copy-start(f32[64]{0:T(128)} %custom-call.1) | copy-start | bytes 772
  29.0 16.0 %copy-start.15 = (pred[128]{0:T(512)(128)(4,1)S(1)}, pred[128]{0:T(512)(128)(4,1)}, u32[]{:S(2)}) copy-start(pred[128]{0:T(512)(128)(4,1)} %get-tuple-element.283) | copy-start | bytes 388
  40.5 4.5 copy-start.5
  40.5 29.6 %copy-start.3 = (f32[128,4096]{1,0:T(8,128)S(1)}, f32[128,4096]{1,0:T(8,128)}, u32[]{:S(2)}) copy-start(f32[128,4096]{1,0:T(8,128)} %copy.80) | copy-start | bytes 6291460
  40.5 26.5 %all-to-all-start = ((bf16[1,4,1,32,4096]{4,3,2,0,1:T(8,128)(2,1)}), bf16[1,4,1,32,4096]{4,3,2,0,1:T(8,128)(2,1)S(1)}, u32[]{:S(2)}, u32[]{:S(2)}) async-start(bf16[1,4,1,32,4096]{4,3,2,0,1:T(8,128)(2,1)} %bitcast.135), calls=%async_computation | async-start | bytes 2097152 | tf_op jit(solution)/shard_map/all_to_all | solution.py:108
  44.2 197.7 %all-gather.10.cloned.1.call-start = ((), (), s32[]{:S(2)}) async-start(), calls=%async_computation.7 | async-start | bytes 10485760 | tf_op jit(solution)/shard_map/all_gather | solution.py:23
  45.0 22.0 %copy-start.7 = (f32[64]{0:T(128)}, f32[64]{0:T(128)S(1)}, u32[]{:S(2)}) copy-start(f32[64]{0:T(128)S(1)} %get-tuple-element.224) | copy-start | bytes 772
  45.0 22.0 %copy-start.10 = (f32[4,64]{1,0:T(4,128)}, f32[4,64]{1,0:T(4,128)S(1)}, u32[]{:S(2)}) copy-start(f32[4,64]{1,0:T(4,128)S(1)} %get-tuple-element.430) | copy-start | bytes 3076
  46.6 22.0 %collective-permute-start.1 = (bf16[3,256]{1,0:T(4,128)(2,1)S(1)}, bf16[3,256]{1,0:T(4,128)(2,1)S(1)}, u32[]{:S(2)}, u32[]{:S(2)}) collective-permute-start(bf16[3,256]{1,0:T(4,128)(2,1)S(1)} %get-tuple-element.287), channel_id=1, source_target_pairs={{0,4},{4,8},{8,12},{1,5},{5,9},{9,13},{2,6},{6,10},{10,14},{3,7},{... | collective-permute-start | bytes 4616 | tf_op jit(solution)/shard_map/ppermute | solution.py:18
  67.3 2.9 collective-permute-start
  68.6 0.6 copy-start.16
  73.3 1.6 copy-start.8
  73.3 1.6 copy-start.17
  77.3 5.7 %copy-start.12 = (f32[128]{0:T(128)S(1)}, f32[128]{0:T(128)}, u32[]{:S(2)}) copy-start(f32[128]{0:T(128)} %copy-done.11) | copy-start | bytes 1540
  77.3 5.8 %copy-start.14 = (f32[64]{0:T(128)S(1)}, f32[64]{0:T(128)}, u32[]{:S(2)}) copy-start(f32[64]{0:T(128)} %param.22) | copy-start | bytes 772
  77.3 54.5 %all-to-all-start.3 = ((bf16[1,4,1,32,4096]{4,3,2,0,1:T(8,128)(2,1)}), bf16[1,4,1,32,4096]{4,3,2,0,1:T(8,128)(2,1)}, u32[]{:S(2)}, u32[]{:S(2)}) async-start(bf16[1,4,1,32,4096]{4,3,2,0,1:T(8,128)(2,1)} %bitcast.35), calls=%async_computation.3 | async-start | bytes 2097152 | tf_op jit(solution)/shard_map/all_to_all | solution.py:109
  83.0 247.5 %all-reduce.3.cloned.1.call-start = ((), (), s32[]{:S(2)}) async-start(), calls=%async_computation.6 | async-start | bytes 4194304 | tf_op jit(solution)/shard_map/psum | solution.py:174
  149.9 1.2 copy-start.4
  150.0 214.3 %all-gather.6.cloned.1.call-start = ((), (), s32[]{:S(2)}) async-start(), calls=%async_computation.4 | async-start | bytes 3145728 | tf_op jit(solution)/shard_map/all_gather | solution.py:182
  241.9 11.4 %copy-start.18 = (f32[64]{0:T(128)S(1)}, f32[64]{0:T(128)}, u32[]{:S(2)}) copy-start(f32[64]{0:T(128)} %param.23) | copy-start | bytes 772
  259.1 8.0 %copy-start.2 = (f32[1,4,1,32,4096]{4,3,1,2,0:T(8,128)S(1)}, f32[1,4,1,32,4096]{4,3,1,2,0:T(8,128)}, u32[]{:S(2)}) copy-start(f32[1,4,1,32,4096]{4,3,1,2,0:T(8,128)} %bitcast_convert_fusion) | copy-start | bytes 6291460
  259.1 8.0 %copy-start.9 = (f32[4096]{0:T(1024)S(1)}, f32[4096]{0:T(1024)}, u32[]{:S(2)}) copy-start(f32[4096]{0:T(1024)} %param.26) | copy-start | bytes 49156
  270.4 0.7 copy-start.19
  270.4 3.2 copy-start.13
  270.4 246.4 %all-gather.8.cloned.1.call-start = ((), (), s32[]{:S(2)}) async-start(), calls=%async_computation.5 | async-start | bytes 18874368 | tf_op jit(solution)/shard_map/all_gather | solution.py:184
  516.8 9.5 %copy-start.1 = (bf16[1,4,1,32,64]{4,3,2,1,0:T(8,128)(2,1)S(1)}, bf16[1,4,1,32,64]{4,3,2,1,0:T(8,128)(2,1)}, u32[]{:S(2)}) copy-start(bf16[1,4,1,32,64]{4,3,2,1,0:T(8,128)(2,1)} %param.20) | copy-start | bytes 49156
Sparse Core Ops, SparseCore 0:
  77.4 164.3 all-gather.9
  244.2 86.2 all-reduce.2
  332.1 32.1 all-gather.5
  365.7 151.0 all-gather.7
where the time goes:
time: 534 us; the launch traced here: 533 us
  waiting for transfers between devices  374 us (70%)
  local copies, waits for them, and re-layouts  36.1 us (7%)
  blocking collectives  34.7 us (6%)
  starting transfers between devices  25.4 us (5%)
  other arithmetic  24.6 us (5%)
  matrix products  21.1 us (4%)
  between operations  16.6 us (3%)
    all_gather x1, waiting for transfers between devices, local(): lax.all_gather(out_weight, ('seq', 'rep'), axis=0, tiled=True)  153 us
    all_gather x1, waiting for transfers between devices, prefix(): everything = jax.tree.map(lambda part: lax.all_gather(part, axis), value)  87.4 us
    all_to_all x1, waiting for transfers between devices, local(): lax.all_to_all(gate_proj, 'seq', split_axis=1, concat_axis=2, tiled=True)  48.3 us
    psum x1, waiting for transfers between devices, local(): final_state = lax.psum(after_decay[:, None, None] * local_final, 'seq')  37.3 us
    all_gather x1, waiting for transfers between devices, local(): features = lax.all_gather(normed, 'head', axis=1, tiled=True)  30.6 us
    psum x1, blocking collectives, broadcast(): return lax.psum(block, axis)  18.3 us
    all_to_all x1, waiting for transfers between devices, local(): lax.all_to_all(x_proj, 'seq', split_axis=1, concat_axis=2, tiled=True)  16.6 us
    all_gather x1, blocking collectives, prefix(): everything = jax.tree.map(lambda part: lax.all_gather(part, axis), value)  11.5 us
  transfers between devices with their start and end apart: 10, of which 8 were waited for; matrix products, arithmetic and copies ran while one was open for 12% of the time, Pallas kernels for 0%

commit v1 on v0

--- a/solution.py
+++ b/solution.py
@@ -179,7 +179,8 @@
     ssm_state = take_slab(final_state.reshape(heads, -1), slab_index, seq_count)[None, None]
     conv_x_state = take_slab(keep_x, slab_index, seq_count)[None, None]
     conv_bc_state = take_slab(keep_bc, slab_index, seq_count)[None, None]
-    features = lax.all_gather(normed, "head", axis=1, tiled=True)
+    shards = lax.all_gather(normed, "head", axis=0, tiled=False)
+    features = jnp.concatenate(shards, axis=1)
     out_cols = out_weight.shape[1]
     mixed_sum = add_rows(features, lax.all_gather(out_weight, ("seq", "rep"), axis=0, tiled=True))
     mixed = mixed_sum.astype(jnp.bfloat16).reshape(1, tokens_here, out_cols)

time: 534 us -> 532 us (level)
  no operation moved by 1% of the time
where the time goes in v1:
time: 532 us; the launch traced here: 530 us
  waiting for transfers between devices  372 us (70%)
  local copies, waits for them, and re-layouts  37.8 us (7%)
  blocking collectives  34.7 us (7%)
  starting transfers between devices  25.4 us (5%)
  other arithmetic  23.4 us (4%)
  matrix products  20.5 us (4%)
  between operations  16.6 us (3%)
    all_gather x1, waiting for transfers between devices, local(): lax.all_gather(out_weight, ('seq', 'rep'), axis=0, tiled=True)  149 us
    all_gather x1, waiting for transfers between devices, prefix(): everything = jax.tree.map(lambda part: lax.all_gather(part, axis), value)  88.3 us
    all_to_all x1, waiting for transfers between devices, local(): lax.all_to_all(gate_proj, 'seq', split_axis=1, concat_axis=2, tiled=True)  48.2 us
    psum x1, waiting for transfers between devices, local(): final_state = lax.psum(after_decay[:, None, None] * local_final, 'seq')  37.4 us
    all_gather x1, waiting for transfers between devices, local(): shards = lax.all_gather(normed, 'head', axis=0, tiled=False)  30.6 us
    psum x1, blocking collectives, broadcast(): return lax.psum(block, axis)  18.3 us
    all_to_all x1, waiting for transfers between devices, local(): lax.all_to_all(x_proj, 'seq', split_axis=1, concat_axis=2, tiled=True)  16.7 us
    all_gather x1, blocking collectives, prefix(): everything = jax.tree.map(lambda part: lax.all_gather(part, axis), value)  11.5 us
  transfers between devices with their start and end apart: 10, of which 8 were waited for; matrix products, arithmetic and copies ran while one was open for 12% of the time, Pallas kernels for 0%

profile of v1, /device:TPU:0, one launch (start us, length us, event | category | flops | bytes accessed | tf_op | source)
XLA Modules:
  0.0 530.5 jit_solution(8030545253947052130)
XLA Ops:
  8.6 6.3 %all-to-all-start.2 = ((bf16[4,2,1024]{2,1,0:T(2,128)(2,1)}), bf16[4,2,1024]{2,1,0:T(2,128)(2,1)S(1)}, u32[]{:S(2)}, u32[]{:S(2)}) async-start(bf16[4,2,1024]{2,1,0:T(2,128)(2,1)} %reshape.544), calls=%async_computation.2 | async-start | bytes 32768 | tf_op jit(solution)/shard_map/all_to_all | solution.py:111
  20.6 4.5 all-to-all-start.1
  29.0 11.5 %all-gather = f32[4,1,64]{2,1,0:T(1,128)S(1)} all-gather(f32[1,1,64]{2,1,0:T(1,128)S(1)} %get-tuple-element.290), channel_id=2, replica_groups=mesh['grp'=2,'seq'=4,'head'=2,'rep'=2] {'seq'}, dimensions={0}, use_global_device_ids=true | all-gather | bytes 1280 | tf_op jit(solution)/shard_map/all_gather | solution.py:23
  40.5 3.7 all-to-all-start
  46.5 3.8 collective-permute-start.1
  50.3 16.7 %all-to-all-done = bf16[1,4,1,32,4096]{4,3,2,0,1:T(8,128)(2,1)S(1)} async-done(((bf16[1,4,1,32,4096]{4,3,2,0,1:T(8,128)(2,1)}), bf16[1,4,1,32,4096]{4,3,2,0,1:T(8,128)(2,1)S(1)}, u32[]{:S(2)}, u32[]{:S(2)}) %all-to-all-start) | async-done | bytes 1048608 | tf_op jit(solution)/shard_map/all_to_all | solution.py:108
  70.1 3.1 multiply_convert_fusion.3
  73.9 2.4 broadcast_multiply_fusion
  76.3 5.7 %all-to-all-start.3 = ((bf16[1,4,1,32,4096]{4,3,2,0,1:T(8,128)(2,1)}), bf16[1,4,1,32,4096]{4,3,2,0,1:T(8,128)(2,1)S(1)}, u32[]{:S(2)}, u32[]{:S(2)}) async-start(bf16[1,4,1,32,4096]{4,3,2,0,1:T(8,128)(2,1)} %bitcast.35), calls=%async_computation.3 | async-start | bytes 2097152 | tf_op jit(solution)/shard_map/all_to_all | solution.py:109
  82.5 48.2 %all-to-all-done.3 = bf16[1,4,1,32,4096]{4,3,2,0,1:T(8,128)(2,1)S(1)} async-done(((bf16[1,4,1,32,4096]{4,3,2,0,1:T(8,128)(2,1)}), bf16[1,4,1,32,4096]{4,3,2,0,1:T(8,128)(2,1)S(1)}, u32[]{:S(2)}, u32[]{:S(2)}) %all-to-all-start.3) | async-done | bytes 1048608 | tf_op jit(solution)/shard_map/all_to_all | solution.py:109
  130.7 3.3 reshape.539
  134.0 4.8 copy.87
  140.4 2.4 copy.73
  144.4 2.9 reshape_reshape.3
  148.6 3.3 fusion.1
  151.8 88.3 %all-gather.10.cloned.1.call-done = f32[256,64,128]{2,1,0:T(8,128)} async-done(((f32[64,64,128]{2,1,0:T(8,128)}), f32[256,64,128]{2,1,0:T(8,128)}) %all-gather.10.cloned.1.call-update) | async-done | bytes 8388624 | tf_op jit(solution)/shard_map/all_gather | solution.py:23
  240.1 11.4 %while.35 = (s32[]{:T(128)}, f32[64,64,128]{2,1,0:T(8,128)S(1)}, s32[]{:T(128)}, f32[4,64]{1,0:T(4,128)}, f32[4,64,64,128]{3,2,1,0:T(8,128)}, /*index=5*/s32[]{:T(128)}, s32[]{:T(128)}) while((s32[]{:T(128)}, f32[64,64,128]{2,1,0:T(8,128)S(1)}, s32[]{:T(128)}, f32[4,64]{1,0:T(4,128)}, f32[4,64,64,128]{3,2,1,0:T(8,128)}, ...), condition=%wide.region_2.3_spmd.clone, body=%wide.region_1.2_spmd.clone.sunk | while | flops 2097156 | bytes 6292329 | solution.py:36
  240.8 2.1 fusion.37
  243.6 2.1 fusion.37
  246.4 2.3 fusion.37
  249.4 2.1 fusion.37
  251.5 5.8 %multiply_reduce_fusion = (f32[128]{0:T(128)S(1)}, f32[1,128,64,64]{1,3,2,0:T(8,128)}) fusion(f32[1,128,64,64]{1,3,2,0:T(8,128)} %copy.87, f32[1,128,64,64]{1,3,2,0:T(8,128)} %bitcast.118, f32[64]{0:T(128)S(1)} %copy-done.19, f32[64,64,128]{2,1,0:T(8,128)S(1)} %get-tuple-element.223, bf16[128,256]{1,0:T(8,128)(2,1)S(1)} %multiply_convert_fusion.5, ...), kind=kOutput, calls=%fused_computation.10 | convolution fusion | flops 811073408 | bytes 10552320 | tf_op jit(solution)/shard_map/kqn,khpn->kqhp/dot_general | solution.py:162
  257.3 3.1 copy.85
  260.4 4.9 psum.28
  265.3 3.3 multiply_convert_fusion.2
  271.9 18.3 %all-reduce = (bf16[3,4,1024]{2,0,1:T(4,128)(2,1)S(1)}, bf16[3,4,64]{2,0,1:T(4,128)(2,1)S(1)}) all-reduce(bf16[3,4,1024]{2,0,1:T(4,128)(2,1)S(1)} %bitcast.125, bf16[3,4,64]{2,0,1:T(4,128)(2,1)S(1)} %copy.90), channel_id=1, replica_groups=mesh['grp'=2,'seq'=4,'head'=2,'rep'=2] {'seq'}, use_global_device_ids=true, to_apply=%region_9.10 | all-reduce | flops 13056 | bytes 52224 | tf_op jit(solution)/shard_map/psum | solution.py:41
  291.4 37.4 %all-reduce.3.cloned.1.call-done = f32[64,4,2048]{2,1,0:T(4,128)} async-done(((f32[64,4,2048]{2,1,0:T(4,128)}), f32[64,4,2048]{2,1,0:T(4,128)}) %all-reduce.3.cloned.1.call-update) | async-done | bytes 2097168 | tf_op jit(solution)/shard_map/psum | solution.py:174
  328.8 2.1 constant_dynamic-slice_fusion
  331.9 30.6 %all-gather.6.cloned.1.call-done = bf16[2,128,4096]{2,1,0:T(8,128)(2,1)} async-done(((bf16[1,128,4096]{2,1,0:T(8,128)(2,1)}), bf16[2,128,4096]{2,1,0:T(8,128)(2,1)}) %all-gather.6.cloned.1.call-update) | async-done | bytes 2097168 | tf_op jit(solution)/shard_map/all_gather | solution.py:182
  362.5 3.1 copy.88
  365.7 149.4 %all-gather.8.cloned.1.call-done = bf16[8192,1024]{1,0:T(8,128)(2,1)} async-done(((bf16[1024,1024]{1,0:T(8,128)(2,1)}), bf16[8192,1024]{1,0:T(8,128)(2,1)}) %all-gather.8.cloned.1.call-update) | async-done | bytes 16777232 | tf_op jit(solution)/shard_map/all_gather | solution.py:185
  515.1 8.8 %fusion.9 = bf16[1,128,1024]{2,1,0:T(8,128)(2,1)} fusion(bf16[128,8192]{0,1:T(8,128)(2,1)S(1)} %bitcast.114, bf16[8192,1024]{1,0:T(8,128)(2,1)} %all-gather.8.cloned.1.call-done), kind=kOutput, calls=%fused_computation.23 | convolution fusion | flops 2147614720 | bytes 19136512 | tf_op jit(solution)/shard_map/dot_general | solution.py:84
  (102 shorter events, 27.6 us)
Async XLA Ops:
  7.2 0.8 copy-start
  8.6 12.0 %all-to-all-start.2 = ((bf16[4,2,1024]{2,1,0:T(2,128)(2,1)}), bf16[4,2,1024]{2,1,0:T(2,128)(2,1)S(1)}, u32[]{:S(2)}, u32[]{:S(2)}) async-start(bf16[4,2,1024]{2,1,0:T(2,128)(2,1)} %reshape.544), calls=%async_computation.2 | async-start | bytes 32768 | tf_op jit(solution)/shard_map/all_to_all | solution.py:111
  19.3 7.5 %copy-start.12 = (f32[128]{0:T(128)}, f32[128]{0:T(128)S(1)}, u32[]{:S(2)}) copy-start(f32[128]{0:T(128)S(1)} %get-tuple-element.282) | copy-start | bytes 1540
  20.6 19.9 %all-to-all-start.1 = ((bf16[1,4,1,32,256]{4,3,2,0,1:T(8,128)(2,1)}), bf16[1,4,1,32,256]{4,3,2,0,1:T(8,128)(2,1)S(1)}, u32[]{:S(2)}, u32[]{:S(2)}) async-start(bf16[1,4,1,32,256]{4,3,2,0,1:T(8,128)(2,1)} %bitcast.130), calls=%async_computation.1 | async-start | bytes 131072 | tf_op jit(solution)/shard_map/all_to_all | solution.py:110
  29.0 15.8 %copy-start.7 = (f32[64]{0:T(128)S(1)}, f32[64]{0:T(128)}, u32[]{:S(2)}) copy-start(f32[64]{0:T(128)} %custom-call.1) | copy-start | bytes 772
  29.0 16.0 %copy-start.16 = (pred[128]{0:T(512)(128)(4,1)S(1)}, pred[128]{0:T(512)(128)(4,1)}, u32[]{:S(2)}) copy-start(pred[128]{0:T(512)(128)(4,1)} %get-tuple-element.283) | copy-start | bytes 388
  40.5 4.4 copy-start.6
  40.5 29.6 %copy-start.4 = (f32[128,4096]{1,0:T(8,128)S(1)}, f32[128,4096]{1,0:T(8,128)}, u32[]{:S(2)}) copy-start(f32[128,4096]{1,0:T(8,128)} %copy.81) | copy-start | bytes 6291460
  40.5 26.5 %all-to-all-start = ((bf16[1,4,1,32,4096]{4,3,2,0,1:T(8,128)(2,1)}), bf16[1,4,1,32,4096]{4,3,2,0,1:T(8,128)(2,1)S(1)}, u32[]{:S(2)}, u32[]{:S(2)}) async-start(bf16[1,4,1,32,4096]{4,3,2,0,1:T(8,128)(2,1)} %bitcast.120), calls=%async_computation | async-start | bytes 2097152 | tf_op jit(solution)/shard_map/all_to_all | solution.py:108
  44.1 196.0 %all-gather.10.cloned.1.call-start = ((), (), s32[]{:S(2)}) async-start(), calls=%async_computation.7 | async-start | bytes 10485760 | tf_op jit(solution)/shard_map/all_gather | solution.py:23
  44.9 22.1 %copy-start.8 = (f32[64]{0:T(128)}, f32[64]{0:T(128)S(1)}, u32[]{:S(2)}) copy-start(f32[64]{0:T(128)S(1)} %get-tuple-element.224) | copy-start | bytes 772
  44.9 22.1 %copy-start.11 = (f32[4,64]{1,0:T(4,128)}, f32[4,64]{1,0:T(4,128)S(1)}, u32[]{:S(2)}) copy-start(f32[4,64]{1,0:T(4,128)S(1)} %get-tuple-element.431) | copy-start | bytes 3076
  46.5 22.1 %collective-permute-start.1 = (bf16[3,256]{1,0:T(4,128)(2,1)S(1)}, bf16[3,256]{1,0:T(4,128)(2,1)S(1)}, u32[]{:S(2)}, u32[]{:S(2)}) collective-permute-start(bf16[3,256]{1,0:T(4,128)(2,1)S(1)} %get-tuple-element.287), channel_id=1, source_target_pairs={{0,4},{4,8},{8,12},{1,5},{5,9},{9,13},{2,6},{6,10},{10,14},{3,7},{... | collective-permute-start | bytes 4616 | tf_op jit(solution)/shard_map/ppermute | solution.py:18
  67.2 2.9 collective-permute-start
  68.5 0.6 copy-start.17
  73.2 0.7 copy-start.9
  73.2 0.7 copy-start.18
  76.3 5.7 %copy-start.13 = (f32[128]{0:T(128)S(1)}, f32[128]{0:T(128)}, u32[]{:S(2)}) copy-start(f32[128]{0:T(128)} %copy-done.12) | copy-start | bytes 1540
  76.3 5.8 %copy-start.15 = (f32[64]{0:T(128)S(1)}, f32[64]{0:T(128)}, u32[]{:S(2)}) copy-start(f32[64]{0:T(128)} %param.22) | copy-start | bytes 772
  76.3 54.4 %all-to-all-start.3 = ((bf16[1,4,1,32,4096]{4,3,2,0,1:T(8,128)(2,1)}), bf16[1,4,1,32,4096]{4,3,2,0,1:T(8,128)(2,1)S(1)}, u32[]{:S(2)}, u32[]{:S(2)}) async-start(bf16[1,4,1,32,4096]{4,3,2,0,1:T(8,128)(2,1)} %bitcast.35), calls=%async_computation.3 | async-start | bytes 2097152 | tf_op jit(solution)/shard_map/all_to_all | solution.py:109
  82.0 246.8 %all-reduce.3.cloned.1.call-start = ((), (), s32[]{:S(2)}) async-start(), calls=%async_computation.6 | async-start | bytes 4194304 | tf_op jit(solution)/shard_map/psum | solution.py:174
  140.4 2.4 copy-start.2
  147.3 1.2 copy-start.5
  147.4 215.2 %all-gather.6.cloned.1.call-start = ((), (), s32[]{:S(2)}) async-start(), calls=%async_computation.4 | async-start | bytes 3145728 | tf_op jit(solution)/shard_map/all_gather | solution.py:182
  240.1 11.4 %copy-start.19 = (f32[64]{0:T(128)S(1)}, f32[64]{0:T(128)}, u32[]{:S(2)}) copy-start(f32[64]{0:T(128)} %param.23) | copy-start | bytes 772
  257.3 8.0 %copy-start.3 = (f32[1,4,1,32,4096]{4,3,2,0,1:T(8,128)S(1)}, f32[1,4,1,32,4096]{4,3,2,0,1:T(8,128)}, u32[]{:S(2)}) copy-start(f32[1,4,1,32,4096]{4,3,2,0,1:T(8,128)} %convert_element_type.168) | copy-start | bytes 6291460
  257.3 8.0 %copy-start.10 = (f32[4096]{0:T(1024)S(1)}, f32[4096]{0:T(1024)}, u32[]{:S(2)}) copy-start(f32[4096]{0:T(1024)} %param.26) | copy-start | bytes 49156
  268.6 0.7 copy-start.20
  268.6 3.2 copy-start.14
  268.6 246.5 %all-gather.8.cloned.1.call-start = ((), (), s32[]{:S(2)}) async-start(), calls=%async_computation.5 | async-start | bytes 18874368 | tf_op jit(solution)/shard_map/all_gather | solution.py:185
  515.1 8.8 %copy-start.1 = (bf16[1,4,1,32,64]{4,3,2,1,0:T(8,128)(2,1)S(1)}, bf16[1,4,1,32,64]{4,3,2,1,0:T(8,128)(2,1)}, u32[]{:S(2)}) copy-start(bf16[1,4,1,32,64]{4,3,2,1,0:T(8,128)(2,1)} %param.20) | copy-start | bytes 49156
Sparse Core Ops, SparseCore 0:
  76.4 163.6 all-gather.9
  242.5 86.2 all-reduce.2
  330.4 32.1 all-gather.5
  364.0 151.0 all-gather.7
